TPU v7x, 32 devices: a whole 2x2x4 slice. The times are simulated.
32 devices in a mesh: member: 4 (over y, x), space: 8 (over z, core).
Axes of the slice: x: 2, y: 2, z: 4, core: 2. Of those that a mesh axis runs over, the one named last changes fastest.
Arguments:
- hidden_codes: bfloat16 [8, 256, 23040], P('member', None, 'space'), may hold values from -6 to 6
- w_in: bfloat16 [1024, 256], replicated, may hold values from -0.375 to 0.375
- b_in: float32 [1024], replicated, may hold values from -3 to 3
- w_out: bfloat16 [72, 1024], replicated, may hold values from -0.1875 to 0.1875
- b_out: float32 [72], replicated, may hold values from -3 to 3
- target: bfloat16 [72, 23040], P(None, 'space'), may hold values from -6 to 6
- band_start: int32 [8], P('space'), may hold values from 0 to 14, as said below
Outputs:
- code_sensitivity: bfloat16 [8, 256, 23040], P('member', None, 'space')
- grad_w_in: float32 [1024, 256], replicated
- grad_w_out: float32 [72, 1024], replicated
- grad_b_in: float32 [1024], replicated
Inputs may be any that keep to these rules, and one draw needn't show every extreme that they name: band_start holds each of 0, 2, 4, ... once, in some order.
All inputs are finite; a program needn't handle non-finite values.
Results may differ from a plain program's by a relative error of at most 0.005.
The roundings to bfloat16 on the way count: a program that leaves them out, or rounds other values in their place, can miss the bound.
Values may be sent and summed in bfloat16 or wider, within the bound.
A program may use at most 128 MiB of HBM per device.

v0:
```python
import functools
import math

import jax
import jax.numpy as jnp
from jax import lax
from jax.experimental import pallas as pl
from jax.experimental.pallas import tpu as pltpu
from jax.sharding import PartitionSpec as P

LON = 1440
HB = 256
MESH = pl.DeviceIdType.MESH
NT = (((1,), (1,)), ((), ()))
F32 = jnp.float32
BF16 = jnp.bfloat16
K0 = math.sqrt(2.0 / math.pi)
K1 = K0 * 0.044715


def slope(diff):
    return diff * lax.rsqrt(diff * diff + 0.0625)


def kernel(
    msize,
    ssize,
    cells,
    hid_ref,
    w_in_ref,
    b_in_ref,
    w_out_ref,
    b_out_ref,
    tgt_ref,
    area_ref,
    code_ref,
    gwi_ref,
    gwo_ref,
    gb_ref,
    hid,
    tgt,
    act,
    dgelu,
    fcs,
    fcr,
    dfs,
    dfr,
    acc_i,
    acc_o,
    acc_b,
    half,
    r1,
    s2,
    r2,
    r3,
    full,
    x1s,
    x1r,
    x2s,
    x2r,
    p1,
    p2s,
    p2r,
    p3s,
    p3r,
    p4s,
    p4r,
    p5s,
    p5r,
    w_in_t,
    w_out_t,
    b_in,
    b_out,
    load,
    save,
):
    local = hid_ref.shape[0]
    hidden = w_in_ref.shape[0]
    latent = w_in_ref.shape[1]
    chans = w_out_ref.shape[0]
    width = hid.shape[2]
    blocks = hidden // HB
    members = local * msize
    zsize = ssize // 2
    me = lax.axis_index("member")
    sp = lax.axis_index("space")
    core = lax.rem(sp, 2)
    z = sp // 2
    partner = z * 2 + (1 - core)

    def mpeer(k):
        return lax.rem(me + k, msize)

    def zpeer(k):
        return lax.rem(z + k, zsize) * 2 + core

    barrier = pltpu.get_barrier_semaphore()
    pl.semaphore_signal(barrier, inc=1, device_id=(me, partner), device_id_type=MESH)
    for k in range(1, msize):
        pl.semaphore_signal(barrier, inc=1, device_id=(mpeer(k), sp), device_id_type=MESH)
    for k in range(1, zsize):
        pl.semaphore_signal(barrier, inc=1, device_id=(me, zpeer(k)), device_id_type=MESH)

    last = msize - 1
    rest = cells - last * width

    def span(c):
        return width if c < last else rest

    def fetch(c, m, n, lo):
        return pltpu.make_async_copy(
            hid_ref.at[m, pl.ds(lo, n)], hid.at[c, m, pl.ds(0, n)], load.at[c, m]
        )

    def put(c, m):
        n = span(c)
        return pltpu.make_async_copy(
            hid.at[c, m, pl.ds(0, n)], code_ref.at[m, pl.ds(c * width, n)], save.at[c, m]
        )

    for c in range(msize):
        for m in range(local):
            fetch(c, m, span(c), c * width).start()
    if rest < width:
        hid[last, :, rest:, :] = jnp.zeros((local, width - rest, latent), BF16)
        tgt[last] = jnp.zeros(tgt.shape[1:], BF16)
    for c in range(msize):
        n = span(c)
        tgt[c, :, :n] = tgt_ref[:, c * width : c * width + n]
    b_in[...] = jnp.transpose(jnp.broadcast_to(b_in_ref[...], (128, hidden)))
    b_out[...] = jnp.transpose(jnp.broadcast_to(b_out_ref[...], (128, chans)))
    acc_i[...] = jnp.zeros_like(acc_i)
    acc_o[...] = jnp.zeros_like(acc_o)
    acc_b[...] = jnp.zeros_like(acc_b)

    def x1(k):
        return pltpu.make_async_remote_copy(
            src_ref=fcs.at[mpeer(k)],
            dst_ref=fcr.at[me],
            send_sem=x1s.at[k],
            recv_sem=x1r.at[k],
            device_id=(mpeer(k), sp),
            device_id_type=MESH,
        )

    def x2(k):
        return pltpu.make_async_remote_copy(
            src_ref=dfs.at[mpeer(k)],
            dst_ref=dfr.at[me],
            send_sem=x2s.at[k],
            recv_sem=x2r.at[k],
            device_id=(mpeer(k), sp),
            device_id_type=MESH,
        )

    def forward(c):
        for m in range(local):

            @pl.when(c < last)
            def _():
                fetch(c, m, width, 0).wait()

            @pl.when(c == last)
            def _():
                fetch(c, m, rest, 0).wait()

            def block(h, carry):
                rows = pl.ds(pl.multiple_of(h * HB, HB), HB)
                x = lax.dot_general(
                    w_in_ref[rows, :], hid[c, m], NT, preferred_element_type=F32
                )
                x = x + b_in[rows, :1]
                u = x * x
                s = 0.5 + 0.5 * jnp.tanh(x * (K0 + K1 * u))
                g = x * s
                act[c, m, rows, :] = g.astype(BF16)
                dgelu[c, m, rows, :] = s + (g * (1.0 - s)) * (2.0 * K0 + (6.0 * K1) * u)
                return carry

            lax.fori_loop(0, blocks, block, 0)
            fc = jnp.dot(w_out_ref[...], act[c, m], preferred_element_type=F32)
            fcs[c, m] = (fc + b_out[:, :1]).astype(BF16)

    def step(k, carry):
        forward(mpeer(k))

        @pl.when(k == 1)
        def _():
            pl.semaphore_wait(barrier, msize + zsize - 1)

        x1(k).start()
        return carry

    lax.fori_loop(1, msize, step, 0)
    forward(me)
    fcr[me] = fcs[me]
    w_in_t[...] = jnp.transpose(w_in_ref[...])
    w_out_t[...] = jnp.transpose(w_out_ref[...].astype(F32)).astype(BF16)
    for k in range(1, msize):
        x1(k).wait()

    def pairs(i, carry):
        lanes = pl.ds(pl.multiple_of(i * 128, 128), 128)
        vals = [fcr[q // local, q % local, :, lanes].astype(F32) for q in range(members)]
        total = [jnp.zeros_like(vals[0]) for q in range(members)]
        for a in range(members):
            for b in range(a + 1, members):
                s = slope(vals[a] - vals[b])
                total[a] = total[a] + s
                total[b] = total[b] - s
        goal = tgt[me, :, lanes].astype(F32)
        weight = area_ref[me, :, lanes]
        for q in range(members):
            d = weight * (slope(vals[q] - goal) - total[q] * (1.0 / members))
            dfs[q // local, q % local, :, lanes] = d.astype(BF16)
        return carry

    lax.fori_loop(0, width // 128, pairs, 0)
    for k in range(1, msize):
        x2(k).start()
    dfr[me] = dfs[me]

    def backward(c):
        for m in range(local):
            df = dfr[c, m]

            def block(h, carry):
                rows = pl.ds(pl.multiple_of(h * HB, HB), HB)
                acc_o[rows, :chans] += lax.dot_general(
                    act[c, m, rows, :], df, NT, preferred_element_type=F32
                )
                da = jnp.dot(w_out_t[rows, :], df, preferred_element_type=F32)
                dp = (da * dgelu[c, m, rows, :]).astype(BF16)
                act[c, m, rows, :] = dp
                acc_i[rows, :] += jnp.dot(dp, hid[c, m], preferred_element_type=F32)
                dpf = dp.astype(F32)
                tot = dpf[:, :128]
                for i in range(1, width // 128):
                    tot = tot + dpf[:, i * 128 : (i + 1) * 128]
                acc_b[rows, :] += tot
                return carry

            lax.fori_loop(0, blocks, block, 0)

    backward(me)

    def bstep(k, carry):
        x2(k).wait()
        backward(lax.rem(me + msize - k, msize))
        return carry

    lax.fori_loop(1, msize, bstep, 0)

    todo = [(c, m) for c in range(msize) for m in range(local)]

    def back_to_codes(count):
        for _ in range(min(count, len(todo))):
            c, m = todo.pop(0)
            d = jnp.dot(w_in_t[...], act[c, m], preferred_element_type=F32)
            hid[c, m] = jnp.transpose(d.astype(BF16))
            put(c, m).start()

    nrows = hidden // 2
    piece = nrows // msize

    def collect(start):
        rows = pl.ds(pl.multiple_of(start, nrows), nrows)
        bias = jnp.sum(acc_b[rows, :], axis=1, keepdims=True)
        lane = lax.broadcasted_iota(jnp.int32, (nrows, 128), 1)
        right = jnp.where(lane == chans, bias, 0.0)
        return rows, right

    def right_of(start):
        rows, bias = collect(start)
        return acc_i[rows, :], acc_o[rows, :] + bias

    li, lr = right_of((1 - core) * nrows)
    half[:, :latent] = li.astype(BF16)
    half[:, latent:] = lr.astype(BF16)
    c1 = pltpu.make_async_remote_copy(
        src_ref=half,
        dst_ref=r1,
        send_sem=p1.at[0],
        recv_sem=p1.at[1],
        device_id=(me, partner),
        device_id_type=MESH,
    )
    c1.start()
    back_to_codes(1)
    c1.wait()
    mi, mr = right_of(core * nrows)
    s2[:, :, :latent] = (mi + r1[:, :latent].astype(F32)).astype(BF16).reshape(
        msize, piece, latent
    )
    s2[:, :, latent:] = (mr + r1[:, latent:].astype(F32)).astype(BF16).reshape(
        msize, piece, 128
    )
    moves = []
    for k in range(1, msize):
        moves.append(
            pltpu.make_async_remote_copy(
                src_ref=s2.at[mpeer(k)],
                dst_ref=r2.at[k],
                send_sem=p2s.at[k],
                recv_sem=p2r.at[k],
                device_id=(mpeer(k), sp),
                device_id_type=MESH,
            )
        )
        moves[-1].start()
    back_to_codes(len(todo) // 2)
    for copy in moves:
        copy.wait()
    summed = s2[me].astype(F32)
    for k in range(1, msize):
        summed = summed + r2[k].astype(F32)
    r3[z] = summed.astype(BF16)
    moves = []
    for k in range(1, zsize):
        moves.append(
            pltpu.make_async_remote_copy(
                src_ref=r3.at[z],
                dst_ref=r3.at[z],
                send_sem=p3s.at[k],
                recv_sem=p3r.at[k],
                device_id=(me, zpeer(k)),
                device_id_type=MESH,
            )
        )
        moves[-1].start()
    back_to_codes(len(todo))
    for copy in moves:
        copy.wait()
    summed = r3[0].astype(F32)
    for k in range(1, zsize):
        summed = summed + r3[k].astype(F32)
    full[core, me] = summed.astype(BF16)

    def share(k):
        return pltpu.make_async_remote_copy(
            src_ref=full.at[core, me],
            dst_ref=full.at[core, me],
            send_sem=p4s.at[k],
            recv_sem=p4r.at[k],
            device_id=(mpeer(k), sp),
            device_id_type=MESH,
        )

    def across(k):
        owner = lax.rem(me + msize - k, msize)
        return pltpu.make_async_remote_copy(
            src_ref=full.at[core, owner],
            dst_ref=full.at[core, owner],
            send_sem=p5s.at[k],
            recv_sem=p5r.at[k],
            device_id=(me, partner),
            device_id_type=MESH,
        )

    for k in range(1, msize):
        share(k).start()
    across(0).start()
    for k in range(1, msize):
        share(k).wait()
        across(k).start()
    for k in range(msize):
        across(k).wait()
    scale = 1.0 / math.sqrt(members * cells)
    for side in range(2):
        for m in range(msize):
            lo = side * nrows + m * piece
            gwi_ref[lo : lo + piece, :] = full[side, m, :, :latent].astype(F32) * scale
            acc_o[lo : lo + piece, :] = full[side, m, :, latent:].astype(F32) * scale
    turned = jnp.transpose(acc_o[...])
    gwo_ref[...] = turned[:chans]
    gb_ref[...] = turned[chans : chans + 1]
    for c in range(msize):
        for m in range(local):
            put(c, m).wait()


def on_device(hidden_codes, w_in, b_in, w_out, b_out, target, band_start):
    local, latent, cells = hidden_codes.shape
    hidden = w_in.shape[0]
    chans = w_out.shape[0]
    msize = lax.axis_size("member")
    ssize = lax.axis_size("space")
    zsize = ssize // 2
    rows = cells // LON
    lat_rows = rows * ssize
    tiles = -(-cells // 128)
    width = -(-tiles // msize) * 128
    place = jnp.arange(msize * width, dtype=jnp.int32)
    angle = ((band_start[0] + place // LON).astype(F32) + 0.5) * (
        math.pi / lat_rows
    ) - math.pi / 2
    area = jnp.where(place < cells, jnp.cos(angle), 0.0).reshape(msize, 1, width)
    nrows = hidden // 2
    piece = nrows // msize
    wide = latent + 128
    vmem = pl.BlockSpec(memory_space=pltpu.VMEM)
    dma = pltpu.SemaphoreType.DMA
    code, gwi, gwo, gb = pl.pallas_call(
        functools.partial(kernel, msize, ssize, cells),
        out_shape=(
            jax.ShapeDtypeStruct((local, cells, latent), BF16),
            jax.ShapeDtypeStruct((hidden, latent), F32),
            jax.ShapeDtypeStruct((chans, hidden), F32),
            jax.ShapeDtypeStruct((1, hidden), F32),
        ),
        in_specs=[pl.BlockSpec(memory_space=pl.ANY)] + [vmem] * 6,
        out_specs=(pl.BlockSpec(memory_space=pl.ANY),) + (vmem,) * 3,
        scratch_shapes=[
            pltpu.VMEM((msize, local, width, latent), BF16),
            pltpu.VMEM((msize, chans, width), BF16),
            pltpu.VMEM((msize, local, hidden, width), BF16),
            pltpu.VMEM((msize, local, hidden, width), F32),
            pltpu.VMEM((msize, local, chans, width), BF16),
            pltpu.VMEM((msize, local, chans, width), BF16),
            pltpu.VMEM((msize, local, chans, width), BF16),
            pltpu.VMEM((msize, local, chans, width), BF16),
            pltpu.VMEM((hidden, latent), F32),
            pltpu.VMEM((hidden, 128), F32),
            pltpu.VMEM((hidden, 128), F32),
            pltpu.VMEM((nrows, wide), BF16),
            pltpu.VMEM((nrows, wide), BF16),
            pltpu.VMEM((msize, piece, wide), BF16),
            pltpu.VMEM((msize, piece, wide), BF16),
            pltpu.VMEM((zsize, piece, wide), BF16),
            pltpu.VMEM((2, msize, piece, wide), BF16),
            dma((msize,)),
            dma((msize,)),
            dma((msize,)),
            dma((msize,)),
            dma((2,)),
            dma((msize,)),
            dma((msize,)),
            dma((zsize,)),
            dma((zsize,)),
            dma((msize,)),
            dma((msize,)),
            dma((msize,)),
            dma((msize,)),
            pltpu.VMEM((latent, hidden), BF16),
            pltpu.VMEM((hidden, chans), BF16),
            pltpu.VMEM((hidden, 128), F32),
            pltpu.VMEM((chans, 128), F32),
            dma((msize, local)),
            dma((msize, local)),
        ],
        compiler_params=pltpu.CompilerParams(
            collective_id=0, has_side_effects=True, vmem_limit_bytes=67043328
        ),
    )(
        jnp.swapaxes(hidden_codes, 1, 2),
        w_in,
        b_in[None, :],
        w_out,
        b_out[None, :],
        target,
        area,
    )
    return jnp.swapaxes(code, 1, 2), gwi, gwo, gb[0]


def solution(mesh):
    in_specs = (P("member", None, "space"), P(), P(), P(), P(), P(None, "space"), P("space"))
    out_specs = (P("member", None, "space"), P(), P(), P())
    return jax.shard_map(
        on_device, mesh=mesh, in_specs=in_specs, out_specs=out_specs, check_vma=False
    )
```

profile of v0, /device:TPU:0, one launch (start us, length us, event | category | flops | bytes accessed | tf_op | source)
XLA Modules:
  0.0 88.8 jit_solution(12433758501792038973)
XLA Ops:
  1.3 1.0 %compare_select_fusion.area_ref = f32[4,1,768]{2,1,0:T(1,128)} fusion(s32[]{:T(128)} %bitcast.6), kind=kLoop, calls=%fused_computation.1 | loop fusion | flops 52224 | bytes 12292 | tf_op jit(solution)/shard_map/jit(_where)/select_n | solution.py:397
  2.2 80.6 %shard_map.102 = (bf16[2,2880,256]{2,1,0:T(8,128)(2,1)}, f32[1024,256]{1,0:T(8,128)}, f32[72,1024]{1,0:T(8,128)}, f32[1,1024]{1,0:T(1,128)}) custom-call(bf16[2,2880,256]{2,1,0:T(8,128)(2,1)} %bitcast.7, bf16[1024,256]{1,0:T(8,128)(2,1)} %w_in_ref.1, f32[1,1024]{1,0:T(1,128)} %bitcast.9, bf16[72,1024]{1,0:T(8,128)(2,1)} %w_out_ref.1, f32[1,72]{1,0:T(1,128)} %bitcast.11, ...), custom_call_target="tpu_custom_call" | custom-call | tf_op jit(solution)/shard_map/pallas_call | solution.py:403
  82.8 0.0 copy-start
  82.8 0.0 copy-start.1
  82.8 0.0 copy-start.2
  82.8 3.7 %copy.16 = bf16[2,256,2880]{1,2,0:T(8,128)(2,1)} copy(bf16[2,256,2880]{1,2,0:T(8,128)(2,1)} %bitcast.8) | data formatting | bytes 5898240
  86.5 0.0 copy-done
  86.6 1.0 %copy.17 = f32[1024,256]{1,0:T(8,128)} copy(f32[1024,256]{1,0:T(8,128)S(1)} %copy-done) | data formatting | bytes 2097152
  87.5 0.0 copy-done.1
  87.5 0.7 copy.18
  88.2 0.0 copy-done.2
  88.2 0.6 copy.19
Async XLA Ops:
  82.8 3.8 %copy-start = (f32[1024,256]{1,0:T(8,128)S(1)}, f32[1024,256]{1,0:T(8,128)}, u32[]{:S(2)}) copy-start(f32[1024,256]{1,0:T(8,128)} %get-tuple-element.17) | copy-start | bytes 3145732
  82.8 4.7 %copy-start.1 = (f32[72,1024]{1,0:T(8,128)S(1)}, f32[72,1024]{1,0:T(8,128)}, u32[]{:S(2)}) copy-start(f32[72,1024]{1,0:T(8,128)} %get-tuple-element.18) | copy-start | bytes 884740
  82.8 5.4 %copy-start.2 = (f32[1,1024]{1,0:T(1,128)S(1)}, f32[1,1024]{1,0:T(1,128)}, u32[]{:S(2)}) copy-start(f32[1,1024]{1,0:T(1,128)} %get-tuple-element.11) | copy-start | bytes 12292
where the time goes:
time: 89 us; the launch traced here: 88.8 us
  Pallas kernels  80.6 us (91%)
  local copies, waits for them, and re-layouts  6.01 us (7%)
  between operations  1.31 us (1%)
  other arithmetic  0.96 us (1%)
    pallas_call x1, Pallas kernels, on_device(): pl.pallas_call(functools.partial(kernel, msize, ssize, cells), out_shape=...  80.6 us
    unnamed x10, local copies, waits for them, and re-layouts  6.01 us

commit v1 on v0

v1 whole, which is shorter than its diff:
```python
import functools
import math

import jax
import jax.numpy as jnp
from jax import lax
from jax.experimental import pallas as pl
from jax.experimental.pallas import tpu as pltpu
from jax.sharding import PartitionSpec as P

LON = 1440
BR = 256
MESH = pl.DeviceIdType.MESH
NT = (((1,), (1,)), ((), ()))
F32 = jnp.float32
BF16 = jnp.bfloat16
K0 = math.sqrt(2.0 / math.pi)
K1 = K0 * 0.044715


def slope(diff):
    return diff * lax.rsqrt(diff * diff + 0.0625)


def gelu_slope(h):
    q = h * h
    t = jnp.tanh(h * (2.0 * K0 + (8.0 * K1) * q))
    v = (1.0 - t) * (h * (2.0 * K0 + (24.0 * K1) * q))
    return (1.0 + t) * (1.0 + v)


def kernel(
    msize,
    ssize,
    cells,
    hid_ref,
    w_in_ref,
    b_in_ref,
    w_out_ref,
    b_out_ref,
    tgt_ref,
    start_ref,
    code_ref,
    gwi_ref,
    gwo_ref,
    gb_ref,
    tgt,
    area,
    act,
    pre,
    fcs,
    fcr,
    dfr,
    acc_i,
    acc_o,
    acc_b,
    half,
    r1,
    s2,
    r2,
    r3,
    full,
    x1s,
    x1r,
    x2s,
    x2r,
    p1s,
    p1r,
    p2s,
    p2r,
    p3s,
    p3r,
    p4s,
    p4r,
    p5s,
    p5r,
    w_half,
    w_in_t,
    w_out_t,
    b_in,
    b_out,
    load,
):
    local = hid_ref.shape[0]
    hidden = w_in_ref.shape[0]
    latent = w_in_ref.shape[1]
    chans = w_out_ref.shape[0]
    width = tgt.shape[2]
    dfs = fcs
    members = local * msize
    zsize = ssize // 2
    ysize = msize // 2
    nb = hidden // BR
    hr = BR // 2
    pr = hr // msize
    parts = x2s.shape[1]
    me = lax.axis_index("member")
    sp = lax.axis_index("space")
    core = lax.rem(sp, 2)
    z = sp // 2
    partner = z * 2 + (1 - core)
    mx = lax.rem(me, 2)
    my = me // 2

    def mpeer(k):
        return lax.rem(my + k // 2, ysize) * 2 + lax.rem(mx + k, 2)

    def mfrom(k):
        return lax.rem(my + ysize - k // 2, ysize) * 2 + lax.rem(mx + k, 2)

    def zpeer(k):
        return lax.rem(z + k, zsize) * 2 + core

    barrier = pltpu.get_barrier_semaphore()
    pl.semaphore_signal(barrier, inc=1, device_id=(me, partner), device_id_type=MESH)
    for k in range(1, msize):
        pl.semaphore_signal(barrier, inc=1, device_id=(mpeer(k), sp), device_id_type=MESH)
    for k in range(1, zsize):
        pl.semaphore_signal(barrier, inc=1, device_id=(me, zpeer(k)), device_id_type=MESH)

    last = msize - 1
    rest = cells - last * width

    def span(c):
        return width if c < last else rest

    def fetch(c, m, n, lo):
        return pltpu.make_async_copy(
            hid_ref.at[m, pl.ds(lo, n)], code_ref.at[m, pl.ds(lo, n)], load.at[c, m]
        )

    def codes(c, m):
        return code_ref[m, pl.ds(pl.multiple_of(c * width, width), width), :]

    for k in range(msize - 1, -1, -1):
        first = mpeer(k)

        @pl.when(first < last)
        def _():
            for m in range(local):
                fetch(first, m, width, pl.multiple_of(first * width, width)).start()

        @pl.when(first == last)
        def _():
            for m in range(local):
                fetch(last, m, rest, last * width).start()

    if rest < width:
        code_ref[:, cells:, :] = jnp.zeros((local, width - rest, latent), BF16)
        tgt[last] = jnp.zeros(tgt.shape[1:], BF16)
    b_in[...] = jnp.transpose(jnp.broadcast_to(b_in_ref[...] * 0.5, (128, hidden)))
    b_out[...] = jnp.transpose(jnp.broadcast_to(b_out_ref[...], (128, chans)))
    w_half[...] = w_in_ref[...] * 0.5

    def x1(k, m):
        return pltpu.make_async_remote_copy(
            src_ref=fcs.at[mpeer(k), m],
            dst_ref=fcr.at[me, m],
            send_sem=x1s.at[k, m],
            recv_sem=x1r.at[k, m],
            device_id=(mpeer(k), sp),
            device_id_type=MESH,
        )

    share_lanes = width // parts

    def x2(k, p):
        lanes = pl.ds(p * share_lanes, share_lanes)
        return pltpu.make_async_remote_copy(
            src_ref=dfs.at[mpeer(k), :, :, lanes],
            dst_ref=dfr.at[me, :, :, lanes],
            send_sem=x2s.at[k, p],
            recv_sem=x2r.at[k, p],
            device_id=(mpeer(k), sp),
            device_id_type=MESH,
        )

    def ready(c):
        for m in range(local):

            @pl.when(c < last)
            def _():
                fetch(c, m, width, 0).wait()

            @pl.when(c == last)
            def _():
                fetch(c, m, rest, 0).wait()

    def forward(c, m):
        x = lax.dot_general(w_half[...], codes(c, m), NT, preferred_element_type=F32)
        h = x + b_in[:, :1]
        pre[c, m] = h
        t = jnp.tanh(h * (2.0 * K0 + (8.0 * K1) * (h * h)))
        act[c, m] = (h + h * t).astype(BF16)
        fc = jnp.dot(w_out_ref[...], act[c, m], preferred_element_type=F32)
        fcs[c, m] = (fc + b_out[:, :1]).astype(BF16)

    def step(i, carry):
        k = msize - 1 - i
        c = mpeer(k)
        with jax.named_scope("fwd"):
            ready(c)
            for m in range(local):
                forward(c, m)

            @pl.when(i == 0)
            def _():
                pl.semaphore_wait(barrier, msize + zsize - 1)

            for m in range(local):
                x1(k, m).start()
        return carry

    lax.fori_loop(0, msize - 1, step, 0)
    with jax.named_scope("fwdme"):
        ready(me)
        for m in range(local):
            forward(me, m)
    fcr[me] = fcs[me]

    def slopes(c, m):
        def block(i, carry):
            rows = pl.ds(pl.multiple_of(i * 128, 128), 128)
            pre[c, m, rows, :] = gelu_slope(pre[c, m, rows, :])
            return carry

        lax.fori_loop(0, hidden // 128, block, 0)

    work = [(k, m) for k in range(msize - 1) for m in range(local)]
    early = 3

    with jax.named_scope("gap1"):
        place = me * width + lax.broadcasted_iota(jnp.int32, (1, width), 1)
        row = jnp.zeros((1, width), jnp.int32) + start_ref[0]
        for r in range(1, cells // LON):
            row = row + jnp.where(place >= r * LON, 1, 0)
        angle = (row.astype(F32) + 0.5) * (math.pi / (cells // LON * ssize)) - math.pi / 2
        area[...] = jnp.where(place < cells, jnp.cos(angle), 0.0)
        acc_i[...] = jnp.zeros_like(acc_i)
        acc_o[...] = jnp.zeros_like(acc_o)
        acc_b[...] = jnp.zeros_like(acc_b)
        for c in range(msize):
            n = span(c)
            tgt[c, :, :n] = tgt_ref[:, c * width : c * width + n]
        w_in_t[...] = jnp.transpose(w_in_ref[...])
        w_out_t[...] = jnp.transpose(w_out_ref[...].astype(F32) * 0.5).astype(BF16)
        for k, m in work[:early]:
            slopes(mfrom(k), m)
    with jax.named_scope("x1wait"):
        for k in range(1, msize):
            for m in range(local):
                x1(k, m).wait()

    def pairs(i, carry):
        lanes = pl.ds(pl.multiple_of(i * 128, 128), 128)
        vals = [fcr[q // local, q % local, :, lanes].astype(F32) for q in range(members)]
        total = [jnp.zeros_like(vals[0]) for q in range(members)]
        for a in range(members):
            for b in range(a + 1, members):
                s = slope(vals[a] - vals[b])
                total[a] = total[a] + s
                total[b] = total[b] - s
        goal = tgt[me, :, lanes].astype(F32)
        weight = area[:, lanes]
        for q in range(members):
            d = weight * (slope(vals[q] - goal) - total[q] * (1.0 / members))
            dfs[q // local, q % local, :, lanes] = d.astype(BF16)
        return carry

    tiles = width // 128 // parts
    with jax.named_scope("pairs"):

        def part(p, carry):
            lax.fori_loop(p * tiles, (p + 1) * tiles, pairs, 0)
            for k in range(1, msize):
                lanes = pl.ds(pl.multiple_of(p * share_lanes, 128), share_lanes)
                pltpu.make_async_remote_copy(
                    src_ref=dfs.at[mpeer(k), :, :, lanes],
                    dst_ref=dfr.at[me, :, :, lanes],
                    send_sem=x2s.at[k, p],
                    recv_sem=x2r.at[k, p],
                    device_id=(mpeer(k), sp),
                    device_id_type=MESH,
                ).start()
            return carry

        lax.fori_loop(0, parts, part, 0)
    dfr[me] = dfs[me]
    with jax.named_scope("gap2"):
        for k, m in work[early:]:
            slopes(mfrom(k), m)

    def backward(c, m, rows, inline):
        df = dfr[c, m]
        acc_o[rows, :chans] += lax.dot_general(
            act[c, m, rows, :], df, NT, preferred_element_type=F32
        )
        da = jnp.dot(w_out_t[rows, :], df, preferred_element_type=F32)
        dg = pre[c, m, rows, :]
        if inline:
            dg = gelu_slope(dg)
        dp = (da * dg).astype(BF16)
        act[c, m, rows, :] = dp
        acc_i[rows, :] += jnp.dot(dp, codes(c, m), preferred_element_type=F32)
        dpf = dp.astype(F32)
        tot = dpf[:, :128]
        for i in range(1, width // 128):
            tot = tot + dpf[:, i * 128 : (i + 1) * 128]
        acc_b[rows, :] += tot

    def arrived(k):
        for p in range(parts):
            x2(k, p).wait()

    def bstep(k, carry):
        @pl.when(k > 0)
        def _():
            with jax.named_scope("x2wait"):
                arrived(k)

        with jax.named_scope("bwd"):
            for m in range(local):
                backward(mfrom(k), m, slice(None), False)
        return carry

    lax.fori_loop(0, msize - 2, bstep, 0)

    with jax.named_scope("x2last"):
        arrived(msize - 2)
        arrived(msize - 1)

    todo = [(c, m) for c in range(msize) for m in range(local)]

    def back_to_codes(count):
        for _ in range(min(count, len(todo))):
            c, m = todo.pop(0)
            with jax.named_scope("dlat"):
                d = jnp.dot(w_in_t[...], act[c, m], preferred_element_type=F32)
                code_ref[m, c * width : (c + 1) * width, :] = jnp.transpose(d.astype(BF16))

    def tail_block(j):
        rows = pl.ds(j * BR, BR)
        with jax.named_scope("bwdlast"):
            for m in range(local):
                for k in (msize - 2, msize - 1):
                    backward(mfrom(k), m, rows, k == msize - 1)

    def side_of(j, side):
        rows = pl.ds(pl.multiple_of(j * BR + side * hr, hr), hr)
        bias = jnp.sum(acc_b[rows, :], axis=1, keepdims=True)
        lane = lax.broadcasted_iota(jnp.int32, (hr, 128), 1)
        return acc_i[rows, :], acc_o[rows, :] + jnp.where(lane == chans, bias, 0.0)

    def c1(j):
        return pltpu.make_async_remote_copy(
            src_ref=half.at[j],
            dst_ref=r1.at[j],
            send_sem=p1s.at[j],
            recv_sem=p1r.at[j],
            device_id=(me, partner),
            device_id_type=MESH,
        )

    def c2(j, k):
        return pltpu.make_async_remote_copy(
            src_ref=s2.at[j, mpeer(k)],
            dst_ref=r2.at[j, k],
            send_sem=p2s.at[j, k],
            recv_sem=p2r.at[j, k],
            device_id=(mpeer(k), sp),
            device_id_type=MESH,
        )

    def c3(j, k):
        return pltpu.make_async_remote_copy(
            src_ref=r3.at[j, z],
            dst_ref=r3.at[j, z],
            send_sem=p3s.at[j, k],
            recv_sem=p3r.at[j, k],
            device_id=(me, zpeer(k)),
            device_id_type=MESH,
        )

    def c4(j, k):
        return pltpu.make_async_remote_copy(
            src_ref=full.at[core, j, me],
            dst_ref=full.at[core, j, me],
            send_sem=p4s.at[j, k],
            recv_sem=p4r.at[j, k],
            device_id=(mpeer(k), sp),
            device_id_type=MESH,
        )

    def c5(j, k):
        owner = mfrom(k)
        return pltpu.make_async_remote_copy(
            src_ref=full.at[core, j, owner],
            dst_ref=full.at[core, j, owner],
            send_sem=p5s.at[j, k],
            recv_sem=p5r.at[j, k],
            device_id=(me, partner),
            device_id_type=MESH,
        )

    def stage1(j):
        li, lr = side_of(j, 1 - core)
        half[j, :, :latent] = li.astype(BF16)
        half[j, :, latent:] = lr.astype(BF16)
        c1(j).start()

    def stage2(j):
        mi, mr = side_of(j, core)
        with jax.named_scope(f"w1_{j}"):
            c1(j).wait()
        s2[j, :, :, :latent] = (
            (mi + r1[j, :, :latent].astype(F32)).astype(BF16).reshape(msize, pr, latent)
        )
        s2[j, :, :, latent:] = (
            (mr + r1[j, :, latent:].astype(F32)).astype(BF16).reshape(msize, pr, 128)
        )
        for k in range(1, msize):
            c2(j, k).start()

    def stage3(j):
        with jax.named_scope(f"w2_{j}"):
            for k in range(1, msize):
                c2(j, k).wait()
        summed = s2[j, me].astype(F32)
        for k in range(1, msize):
            summed = summed + r2[j, k].astype(F32)
        r3[j, z] = summed.astype(BF16)
        for k in range(1, zsize):
            c3(j, k).start()

    def stage4(j):
        with jax.named_scope(f"w3_{j}"):
            for k in range(1, zsize):
                c3(j, k).wait()
        summed = r3[j, 0].astype(F32)
        for k in range(1, zsize):
            summed = summed + r3[j, k].astype(F32)
        full[core, j, me] = summed.astype(BF16)
        for k in range(1, msize):
            c4(j, k).start()
        c5(j, 0).start()

    def stage5(j):
        with jax.named_scope(f"w4_{j}"):
            for k in range(1, msize):
                c4(j, k).wait()
                c5(j, k).start()

    scale = 1.0 / math.sqrt(members * cells)

    def stage6(j):
        with jax.named_scope(f"w5_{j}"):
            for k in range(msize):
                c5(j, k).wait()
        for side in range(2):
            lo = j * BR + side * hr
            whole = full[side, j].astype(F32).reshape(hr, latent + 128) * scale
            gwi_ref[lo : lo + hr, :] = whole[:, :latent]
            turned = jnp.transpose(whole[:, latent:])
            gwo_ref[:, lo : lo + hr] = turned[:chans]
            gb_ref[:, lo : lo + hr] = turned[chans : chans + 1]

    for j in range(nb):
        tail_block(j)
        stage1(j)
        if j > 0:
            stage2(j - 1)
    back_to_codes(1)
    stage3(0)
    back_to_codes(1)
    stage2(nb - 1)
    back_to_codes(2)
    stage3(1)
    back_to_codes(2)
    stage3(2)
    back_to_codes(len(todo))
    stage3(3)
    stage4(0)
    stage4(1)
    stage4(2)
    stage5(0)
    stage4(3)
    stage5(1)
    stage6(0)
    stage6(1)
    stage5(2)
    stage5(3)
    stage6(2)
    stage6(3)


def finish(code, gwi, gwo, gb, code_out, gwi_out, gwo_out, gb_out, sems):
    moves = [
        pltpu.make_async_copy(src, dst, sems.at[i])
        for i, (src, dst) in enumerate(
            (
                (code.at[:, pl.ds(0, code_out.shape[1])], code_out),
                (gwi, gwi_out),
                (gwo, gwo_out),
                (gb, gb_out),
            )
        )
    ]
    for move in moves:
        move.start()
    for move in moves:
        move.wait()


def on_device(hidden_codes, w_in, b_in, w_out, b_out, target, band_start):
    local, latent, cells = hidden_codes.shape
    hidden = w_in.shape[0]
    chans = w_out.shape[0]
    msize = lax.axis_size("member")
    ssize = lax.axis_size("space")
    zsize = ssize // 2
    tiles = -(-cells // 128)
    width = -(-tiles // msize) * 128
    nb = hidden // BR
    hr = BR // 2
    pr = hr // msize
    wide = latent + 128
    parts = 2 if (width // 128) % 2 == 0 else 1
    vmem = pl.BlockSpec(memory_space=pltpu.VMEM)
    dma = pltpu.SemaphoreType.DMA
    code, gwi, gwo, gb = pl.pallas_call(
        functools.partial(kernel, msize, ssize, cells),
        out_shape=(
            pltpu.VMEM((local, msize * width, latent), BF16),
            pltpu.VMEM((hidden, latent), F32),
            pltpu.VMEM((chans, hidden), F32),
            pltpu.VMEM((1, hidden), F32),
        ),
        in_specs=[pl.BlockSpec(memory_space=pl.ANY)]
        + [vmem] * 5
        + [pl.BlockSpec(memory_space=pltpu.SMEM)],
        out_specs=(vmem,) * 4,
        scratch_shapes=[
            pltpu.VMEM((msize, chans, width), BF16),
            pltpu.VMEM((1, width), F32),
            pltpu.VMEM((msize, local, hidden, width), BF16),
            pltpu.VMEM((msize, local, hidden, width), F32),
            pltpu.VMEM((msize, local, chans, width), BF16),
            pltpu.VMEM((msize, local, chans, width), BF16),
            pltpu.VMEM((msize, local, chans, width), BF16),
            pltpu.VMEM((hidden, latent), F32),
            pltpu.VMEM((hidden, 128), F32),
            pltpu.VMEM((hidden, 128), F32),
            pltpu.VMEM((nb, hr, wide), BF16),
            pltpu.VMEM((nb, hr, wide), BF16),
            pltpu.VMEM((nb, msize, pr, wide), BF16),
            pltpu.VMEM((nb, msize, pr, wide), BF16),
            pltpu.VMEM((nb, zsize, pr, wide), BF16),
            pltpu.VMEM((2, nb, msize, pr, wide), BF16),
            dma((msize, local)),
            dma((msize, local)),
            dma((msize, parts)),
            dma((msize, parts)),
            dma((nb,)),
            dma((nb,)),
            dma((nb, msize)),
            dma((nb, msize)),
            dma((nb, zsize)),
            dma((nb, zsize)),
            dma((nb, msize)),
            dma((nb, msize)),
            dma((nb, msize)),
            dma((nb, msize)),
            pltpu.VMEM((hidden, latent), BF16),
            pltpu.VMEM((latent, hidden), BF16),
            pltpu.VMEM((hidden, chans), BF16),
            pltpu.VMEM((hidden, 128), F32),
            pltpu.VMEM((chans, 128), F32),
            dma((msize, local)),
        ],
        compiler_params=pltpu.CompilerParams(
            collective_id=0, has_side_effects=True, vmem_limit_bytes=62_000_000
        ),
    )(
        jnp.swapaxes(hidden_codes, 1, 2),
        w_in,
        b_in[None, :],
        w_out,
        b_out[None, :],
        target,
        band_start,
    )
    code, gwi, gwo, gb = pl.pallas_call(
        finish,
        out_shape=(
            jax.ShapeDtypeStruct((local, cells, latent), BF16),
            jax.ShapeDtypeStruct(gwi.shape, F32),
            jax.ShapeDtypeStruct(gwo.shape, F32),
            jax.ShapeDtypeStruct(gb.shape, F32),
        ),
        in_specs=[vmem] * 4,
        out_specs=(pl.BlockSpec(memory_space=pl.ANY),) * 4,
        scratch_shapes=[dma((4,))],
        compiler_params=pltpu.CompilerParams(vmem_limit_bytes=1 << 20),
    )(code, gwi, gwo, gb)
    return jnp.swapaxes(code, 1, 2), gwi, gwo, gb[0]


def solution(mesh):
    in_specs = (P("member", None, "space"), P(), P(), P(), P(), P(None, "space"), P("space"))
    out_specs = (P("member", None, "space"), P(), P(), P())
    return jax.shard_map(
        on_device, mesh=mesh, in_specs=in_specs, out_specs=out_specs, check_vma=False
    )
```

time: 89 us -> 64 us (0.72)
  Pallas kernels: 80.6 us -> 62.3 us
  local copies, waits for them, and re-layouts: 6.01 us -> 0 us
  other arithmetic: 0.96 us -> 0 us
    pallas_call x1, Pallas kernels: 80.6 us -> 60.3 us  [on_device(): pl.pallas_call(functools.partial(kernel, msize, ssize, cells), out_shape=...]
    unnamed x10 -> x0, local copies, waits for them, and re-layouts: 6.01 us -> none
    pallas_call x0 -> x1, Pallas kernels: none -> 2.07 us  [on_device(): pl.pallas_call(finish, out_shape=(jax.ShapeDtypeStruct((local, cells, lat...]
    select_n x1 -> x0, other arithmetic: 0.96 us -> none  [on_device(): jnp.where(place < cells, jnp.cos(angle), 0.0).reshape(msize, 1, width)]
where the time goes in v1:
time: 64 us; the launch traced here: 63.8 us
  Pallas kernels  62.3 us (97%)
  between operations  1.45 us (2%)
    pallas_call x1, Pallas kernels, on_device(): pl.pallas_call(functools.partial(kernel, msize, ssize, cells), out_shape=...  60.3 us
    pallas_call x1, Pallas kernels, on_device(): pl.pallas_call(finish, out_shape=(jax.ShapeDtypeStruct((local, cells, lat...  2.07 us

profile of v1, /device:TPU:0, one launch (start us, length us, event | category | flops | bytes accessed | tf_op | source)
XLA Modules:
  0.0 63.8 jit_solution(18021566101510113203)
XLA Ops:
  1.3 60.3 %shard_map.102 = (bf16[2,3072,256]{2,1,0:T(8,128)(2,1)S(1)}, f32[1024,256]{1,0:T(8,128)S(1)}, f32[72,1024]{1,0:T(8,128)S(1)}, f32[1,1024]{1,0:T(1,128)S(1)}) custom-call(bf16[2,2880,256]{2,1,0:T(8,128)(2,1)} %bitcast.5, bf16[1024,256]{1,0:T(8,128)(2,1)} %w_in_ref.1, f32[1,1024]{1,0:T(1,128)} %bitcast.6, bf16[72,1024]{1,0:T(8,128)(2,1)} %w_out_ref.1, ...), custom_call_target="tpu_custom_call" | custom-call | tf_op jit(solution)/shard_map/pallas_call | solution.py:530
  61.6 2.1 %shard_map.103 = (bf16[2,2880,256]{2,1,0:T(8,128)(2,1)}, f32[1024,256]{1,0:T(8,128)}, f32[72,1024]{1,0:T(8,128)}, f32[1,1024]{1,0:T(1,128)}) custom-call(bf16[2,3072,256]{2,1,0:T(8,128)(2,1)S(1)} %get-tuple-element.12.code, f32[1024,256]{1,0:T(8,128)S(1)} %get-tuple-element.13.gwi, f32[72,1024]{1,0:T(8,128)S(1)} %get-tuple-element.14.gwo, ...), custom_call_target="tpu_custom_call" | custom-call | tf_op jit(solution)/shard_map/pallas_call | solution.py:592

commit v2 on v1

--- a/solution.py
+++ b/solution.py
@@ -54,7 +54,6 @@
     acc_i,
     acc_o,
     acc_b,
-    half,
     r1,
     s2,
     r2,
@@ -85,7 +84,7 @@
     hidden = w_in_ref.shape[0]
     latent = w_in_ref.shape[1]
     chans = w_out_ref.shape[0]
-    width = tgt.shape[2]
+    width = tgt.shape[1]
     dfs = fcs
     members = local * msize
     zsize = ssize // 2
@@ -147,7 +146,7 @@
 
     if rest < width:
         code_ref[:, cells:, :] = jnp.zeros((local, width - rest, latent), BF16)
-        tgt[last] = jnp.zeros(tgt.shape[1:], BF16)
+        tgt[...] = jnp.zeros(tgt.shape, BF16)
     b_in[...] = jnp.transpose(jnp.broadcast_to(b_in_ref[...] * 0.5, (128, hidden)))
     b_out[...] = jnp.transpose(jnp.broadcast_to(b_out_ref[...], (128, chans)))
     w_half[...] = w_in_ref[...] * 0.5
@@ -165,7 +164,7 @@
     share_lanes = width // parts
 
     def x2(k, p):
-        lanes = pl.ds(p * share_lanes, share_lanes)
+        lanes = pl.ds(pl.multiple_of(p * share_lanes, 128), share_lanes)
         return pltpu.make_async_remote_copy(
             src_ref=dfs.at[mpeer(k), :, :, lanes],
             dst_ref=dfr.at[me, :, :, lanes],
@@ -196,27 +195,31 @@
         fcs[c, m] = (fc + b_out[:, :1]).astype(BF16)
 
     def step(i, carry):
-        k = msize - 1 - i
+        k = last - i
         c = mpeer(k)
         with jax.named_scope("fwd"):
             ready(c)
             for m in range(local):
                 forward(c, m)
 
-            @pl.when(i == 0)
-            def _():
-                pl.semaphore_wait(barrier, msize + zsize - 1)
-
+        @pl.when(i == 0)
+        def _():
+            pl.semaphore_wait(barrier, msize + zsize - 1)
+
+        @pl.when(k > 0)
+        def _():
             for m in range(local):
                 x1(k, m).start()
+
         return carry
 
-    lax.fori_loop(0, msize - 1, step, 0)
-    with jax.named_scope("fwdme"):
-        ready(me)
-        for m in range(local):
-            forward(me, m)
+    lax.fori_loop(0, msize, step, 0)
     fcr[me] = fcs[me]
+
+    def fold(k, m):
+        return m == local - 1 and k < msize - 2 if k < msize - 2 else (k, m) in late
+
+    late = ((msize - 1, local - 1),)
 
     def slopes(c, m):
         def block(i, carry):
@@ -226,8 +229,9 @@
 
         lax.fori_loop(0, hidden // 128, block, 0)
 
-    work = [(k, m) for k in range(msize - 1) for m in range(local)]
-    early = 3
+    folded = [(k, m) for k in range(msize) for m in range(local) if fold(k, m)]
+    work = [(k, m) for k in range(msize) for m in range(local) if (k, m) not in folded]
+    early = 2
 
     with jax.named_scope("gap1"):
         place = me * width + lax.broadcasted_iota(jnp.int32, (1, width), 1)
@@ -240,8 +244,11 @@
         acc_o[...] = jnp.zeros_like(acc_o)
         acc_b[...] = jnp.zeros_like(acc_b)
         for c in range(msize):
-            n = span(c)
-            tgt[c, :, :n] = tgt_ref[:, c * width : c * width + n]
+
+            @pl.when(me == c)
+            def _():
+                n = span(c)
+                tgt[:, :n] = tgt_ref[:, c * width : c * width + n]
         w_in_t[...] = jnp.transpose(w_in_ref[...])
         w_out_t[...] = jnp.transpose(w_out_ref[...].astype(F32) * 0.5).astype(BF16)
         for k, m in work[:early]:
@@ -260,7 +267,7 @@
                 s = slope(vals[a] - vals[b])
                 total[a] = total[a] + s
                 total[b] = total[b] - s
-        goal = tgt[me, :, lanes].astype(F32)
+        goal = tgt[:, lanes].astype(F32)
         weight = area[:, lanes]
         for q in range(members):
             d = weight * (slope(vals[q] - goal) - total[q] * (1.0 / members))
@@ -272,29 +279,25 @@
 
         def part(p, carry):
             lax.fori_loop(p * tiles, (p + 1) * tiles, pairs, 0)
-            for k in range(1, msize):
-                lanes = pl.ds(pl.multiple_of(p * share_lanes, 128), share_lanes)
-                pltpu.make_async_remote_copy(
-                    src_ref=dfs.at[mpeer(k), :, :, lanes],
-                    dst_ref=dfr.at[me, :, :, lanes],
-                    send_sem=x2s.at[k, p],
-                    recv_sem=x2r.at[k, p],
-                    device_id=(mpeer(k), sp),
-                    device_id_type=MESH,
-                ).start()
+            for k in range(1, last):
+                x2(k, p).start()
             return carry
 
         lax.fori_loop(0, parts, part, 0)
+        for p in range(parts):
+            x2(last, p).start()
     dfr[me] = dfs[me]
     with jax.named_scope("gap2"):
         for k, m in work[early:]:
             slopes(mfrom(k), m)
 
-    def backward(c, m, rows, inline):
+    def backward(c, m, rows, inner, inline):
         df = dfr[c, m]
-        acc_o[rows, :chans] += lax.dot_general(
-            act[c, m, rows, :], df, NT, preferred_element_type=F32
-        )
+        if inner:
+            outer = lax.dot_general(df, act[c, m, rows, :], NT, preferred_element_type=F32)
+        else:
+            outer = jnp.dot(df, jnp.transpose(act[c, m, rows, :]), preferred_element_type=F32)
+        acc_o[:chans, rows] += outer
         da = jnp.dot(w_out_t[rows, :], df, preferred_element_type=F32)
         dg = pre[c, m, rows, :]
         if inline:
@@ -320,7 +323,7 @@
 
         with jax.named_scope("bwd"):
             for m in range(local):
-                backward(mfrom(k), m, slice(None), False)
+                backward(mfrom(k), m, slice(None), False, m == local - 1)
         return carry
 
     lax.fori_loop(0, msize - 2, bstep, 0)
@@ -338,22 +341,21 @@
                 d = jnp.dot(w_in_t[...], act[c, m], preferred_element_type=F32)
                 code_ref[m, c * width : (c + 1) * width, :] = jnp.transpose(d.astype(BF16))
 
-    def tail_block(j):
-        rows = pl.ds(j * BR, BR)
+    def tail_block(j, k):
+        rows = pl.ds(pl.multiple_of(j * BR, BR), BR)
         with jax.named_scope("bwdlast"):
             for m in range(local):
-                for k in (msize - 2, msize - 1):
-                    backward(mfrom(k), m, rows, k == msize - 1)
+                backward(mfrom(k), m, rows, True, fold(k, m))
 
     def side_of(j, side):
         rows = pl.ds(pl.multiple_of(j * BR + side * hr, hr), hr)
         bias = jnp.sum(acc_b[rows, :], axis=1, keepdims=True)
         lane = lax.broadcasted_iota(jnp.int32, (hr, 128), 1)
-        return acc_i[rows, :], acc_o[rows, :] + jnp.where(lane == chans, bias, 0.0)
+        return acc_i[rows, :], jnp.transpose(acc_o[:, rows]) + jnp.where(lane == chans, bias, 0.0)
 
     def c1(j):
         return pltpu.make_async_remote_copy(
-            src_ref=half.at[j],
+            src_ref=s2.at[j],
             dst_ref=r1.at[j],
             send_sem=p1s.at[j],
             recv_sem=p1r.at[j],
@@ -404,19 +406,18 @@
 
     def stage1(j):
         li, lr = side_of(j, 1 - core)
-        half[j, :, :latent] = li.astype(BF16)
-        half[j, :, latent:] = lr.astype(BF16)
+        s2[j, :, :, :latent] = li.astype(BF16).reshape(msize, pr, latent)
+        s2[j, :, :, latent:] = lr.astype(BF16).reshape(msize, pr, 128)
         c1(j).start()
 
     def stage2(j):
         mi, mr = side_of(j, core)
-        with jax.named_scope(f"w1_{j}"):
-            c1(j).wait()
+        c1(j).wait()
         s2[j, :, :, :latent] = (
-            (mi + r1[j, :, :latent].astype(F32)).astype(BF16).reshape(msize, pr, latent)
+            (mi.reshape(msize, pr, latent) + r1[j, :, :, :latent].astype(F32)).astype(BF16)
         )
         s2[j, :, :, latent:] = (
-            (mr + r1[j, :, latent:].astype(F32)).astype(BF16).reshape(msize, pr, 128)
+            (mr.reshape(msize, pr, 128) + r1[j, :, :, latent:].astype(F32)).astype(BF16)
         )
         for k in range(1, msize):
             c2(j, k).start()
@@ -464,18 +465,23 @@
             gwo_ref[:, lo : lo + hr] = turned[:chans]
             gb_ref[:, lo : lo + hr] = turned[chans : chans + 1]
 
-    for j in range(nb):
-        tail_block(j)
+    def tstep(j, carry):
+        tail_block(j, msize - 2)
+        tail_block(j, msize - 1)
+
+        @pl.when(j > 0)
+        def _():
+            stage2(j - 1)
+
         stage1(j)
-        if j > 0:
-            stage2(j - 1)
-    back_to_codes(1)
+        return carry
+
+    lax.fori_loop(0, nb, tstep, 0)
     stage3(0)
-    back_to_codes(1)
+    back_to_codes(2)
     stage2(nb - 1)
-    back_to_codes(2)
     stage3(1)
-    back_to_codes(2)
+    back_to_codes(3)
     stage3(2)
     back_to_codes(len(todo))
     stage3(3)
@@ -540,7 +546,7 @@
         + [pl.BlockSpec(memory_space=pltpu.SMEM)],
         out_specs=(vmem,) * 4,
         scratch_shapes=[
-            pltpu.VMEM((msize, chans, width), BF16),
+            pltpu.VMEM((chans, width), BF16),
             pltpu.VMEM((1, width), F32),
             pltpu.VMEM((msize, local, hidden, width), BF16),
             pltpu.VMEM((msize, local, hidden, width), F32),
@@ -548,10 +554,9 @@
             pltpu.VMEM((msize, local, chans, width), BF16),
             pltpu.VMEM((msize, local, chans, width), BF16),
             pltpu.VMEM((hidden, latent), F32),
+            pltpu.VMEM((128, hidden), F32),
             pltpu.VMEM((hidden, 128), F32),
-            pltpu.VMEM((hidden, 128), F32),
-            pltpu.VMEM((nb, hr, wide), BF16),
-            pltpu.VMEM((nb, hr, wide), BF16),
+            pltpu.VMEM((nb, msize, pr, wide), BF16),
             pltpu.VMEM((nb, msize, pr, wide), BF16),
             pltpu.VMEM((nb, msize, pr, wide), BF16),
             pltpu.VMEM((nb, zsize, pr, wide), BF16),

time: 64 us -> 62.6 us (0.978)
  Pallas kernels: 62.3 us -> 61 us
    pallas_call x1, Pallas kernels: 60.3 us -> 58.9 us  [on_device(): pl.pallas_call(functools.partial(kernel, msize, ssize, cells), out_shape=...]
where the time goes in v2:
time: 62.6 us; the launch traced here: 62.4 us
  Pallas kernels  61 us (97%)
  between operations  1.45 us (2%)
    pallas_call x1, Pallas kernels, on_device(): pl.pallas_call(functools.partial(kernel, msize, ssize, cells), out_shape=...  58.9 us
    pallas_call x1, Pallas kernels, on_device(): pl.pallas_call(finish, out_shape=(jax.ShapeDtypeStruct((local, cells, lat...  2.07 us

profile of v2, /device:TPU:0, one launch (start us, length us, event | category | flops | bytes accessed | tf_op | source)
XLA Modules:
  0.0 62.4 jit_solution(3492308929381726965)
XLA Ops:
  1.3 58.9 %shard_map.102 = (bf16[2,3072,256]{2,1,0:T(8,128)(2,1)S(1)}, f32[1024,256]{1,0:T(8,128)S(1)}, f32[72,1024]{1,0:T(8,128)S(1)}, f32[1,1024]{1,0:T(1,128)S(1)}) custom-call(bf16[2,2880,256]{2,1,0:T(8,128)(2,1)} %bitcast.5, bf16[1024,256]{1,0:T(8,128)(2,1)} %w_in_ref.1, f32[1,1024]{1,0:T(1,128)} %bitcast.6, bf16[72,1024]{1,0:T(8,128)(2,1)} %w_out_ref.1, ...), custom_call_target="tpu_custom_call" | custom-call | tf_op jit(solution)/shard_map/pallas_call | solution.py:536
  60.2 2.1 %shard_map.103 = (bf16[2,2880,256]{2,1,0:T(8,128)(2,1)}, f32[1024,256]{1,0:T(8,128)}, f32[72,1024]{1,0:T(8,128)}, f32[1,1024]{1,0:T(1,128)}) custom-call(bf16[2,3072,256]{2,1,0:T(8,128)(2,1)S(1)} %get-tuple-element.12.code, f32[1024,256]{1,0:T(8,128)S(1)} %get-tuple-element.13.gwi, f32[72,1024]{1,0:T(8,128)S(1)} %get-tuple-element.14.gwo, ...), custom_call_target="tpu_custom_call" | custom-call | tf_op jit(solution)/shard_map/pallas_call | solution.py:597

commit v3 on v2

--- a/solution.py
+++ b/solution.py
@@ -231,7 +231,7 @@
 
     folded = [(k, m) for k in range(msize) for m in range(local) if fold(k, m)]
     work = [(k, m) for k in range(msize) for m in range(local) if (k, m) not in folded]
-    early = 2
+    early = 3
 
     with jax.named_scope("gap1"):
         place = me * width + lax.broadcasted_iota(jnp.int32, (1, width), 1)
@@ -483,8 +483,9 @@
     stage3(1)
     back_to_codes(3)
     stage3(2)
+    back_to_codes(2)
+    stage3(3)
     back_to_codes(len(todo))
-    stage3(3)
     stage4(0)
     stage4(1)
     stage4(2)

time: 62.6 us -> 62.6 us (level)
  no operation moved by 1% of the time
where the time goes in v3:
time: 62.6 us; the launch traced here: 62.4 us
  Pallas kernels  61 us (97%)
  between operations  1.45 us (2%)
    pallas_call x1, Pallas kernels, on_device(): pl.pallas_call(functools.partial(kernel, msize, ssize, cells), out_shape=...  58.9 us
    pallas_call x1, Pallas kernels, on_device(): pl.pallas_call(finish, out_shape=(jax.ShapeDtypeStruct((local, cells, lat...  2.07 us

profile of v3, /device:TPU:0, one launch (start us, length us, event | category | flops | bytes accessed | tf_op | source)
XLA Modules:
  0.0 62.4 jit_solution(3712464136290670535)
XLA Ops:
  1.3 58.9 %shard_map.102 = (bf16[2,3072,256]{2,1,0:T(8,128)(2,1)S(1)}, f32[1024,256]{1,0:T(8,128)S(1)}, f32[72,1024]{1,0:T(8,128)S(1)}, f32[1,1024]{1,0:T(1,128)S(1)}) custom-call(bf16[2,2880,256]{2,1,0:T(8,128)(2,1)} %bitcast.5, bf16[1024,256]{1,0:T(8,128)(2,1)} %w_in_ref.1, f32[1,1024]{1,0:T(1,128)} %bitcast.6, bf16[72,1024]{1,0:T(8,128)(2,1)} %w_out_ref.1, ...), custom_call_target="tpu_custom_call" | custom-call | tf_op jit(solution)/shard_map/pallas_call | solution.py:537
  60.2 2.1 %shard_map.103 = (bf16[2,2880,256]{2,1,0:T(8,128)(2,1)}, f32[1024,256]{1,0:T(8,128)}, f32[72,1024]{1,0:T(8,128)}, f32[1,1024]{1,0:T(1,128)}) custom-call(bf16[2,3072,256]{2,1,0:T(8,128)(2,1)S(1)} %get-tuple-element.12.code, f32[1024,256]{1,0:T(8,128)S(1)} %get-tuple-element.13.gwi, f32[72,1024]{1,0:T(8,128)S(1)} %get-tuple-element.14.gwo, ...), custom_call_target="tpu_custom_call" | custom-call | tf_op jit(solution)/shard_map/pallas_call | solution.py:598
